TPU v7x, 128 devices: a whole 4x4x4 slice. The times are simulated.
128 devices in a mesh: rep: 4 (over z_hi, core), row: 4 (over x), col: 8 (over z_lo, y).
Axes of the slice: x: 4, y: 4, z: 4 (z_hi: 2, z_lo: 2; z = z_hi * 2 + z_lo), core: 2. Of those that a mesh axis runs over, the one named last changes fastest.
Arguments:
- grad_parts: bfloat16 [4, 16384, 6144], P('rep', ('row', 'col')), may hold values from -0.03125 to 0.03125, as said below
- statistic: float32 [6144, 6144], P('row', 'col'), may hold values from -150 to 150, as said below
Outputs:
- gram_matrix: float32 [6144, 6144], P('row', 'col')
- statistic_next: float32 [6144, 6144], P('row', 'col')
Inputs may be any that keep to these rules, and one draw needn't show every extreme that they name: Every entry of grad_parts has a magnitude between 2^-10 and 2^-5. statistic is symmetric and positive definite.
All inputs are finite; a program needn't handle non-finite values.
Results may differ from a plain program's by a relative error of at most 0.008.
Values may be sent and summed in bfloat16 or wider, within the bound.
A program may use at most 128 MiB of HBM per device.

v0:
```python
import jax
import jax.numpy as jnp
from jax import lax
from jax.sharding import PartitionSpec as P


def shards(grad_parts, statistic):
    own_part = grad_parts[0].astype(jnp.float32)
    summed = lax.psum_scatter(own_part.astype(jnp.bfloat16), "rep", scatter_dimension=0, tiled=True)
    rows_panel = lax.all_to_all(summed, "row", split_axis=1, concat_axis=0, tiled=True)
    cols_panel = lax.all_to_all(summed, "col", split_axis=1, concat_axis=0, tiled=True)
    row_count = lax.axis_size("row")
    col_count = lax.axis_size("col")
    quarter = summed.shape[0]
    right_whole = lax.all_gather(cols_panel, "row", axis=0, tiled=True)
    right_order = (
        right_whole.reshape(row_count, col_count, quarter, -1)
        .transpose(1, 0, 2, 3)
        .reshape(row_count * col_count * quarter, -1)
    )
    partial_tile = lax.dot_general(
        lax.all_gather(rows_panel, "col", axis=0, tiled=True),
        right_order,
        (((0,), (0,)), ((), ())),
        preferred_element_type=jnp.float32,
    )
    portion = lax.psum_scatter(partial_tile, "rep", scatter_dimension=0, tiled=True)
    gram_tile = lax.all_gather(portion, "rep", axis=0, tiled=True)
    return (gram_tile, 0.95 * statistic + 0.05 * gram_tile)


def solution(mesh):
    return jax.shard_map(
        shards,
        mesh=mesh,
        in_specs=(P("rep", ("row", "col"), None), P("row", "col")),
        out_specs=(P("row", "col"), P("row", "col")),
        check_vma=False,
    )
```

profile of v0, /device:TPU:1, one launch (start us, length us, event | category | flops | bytes accessed | tf_op | source)
XLA Modules:
  0.0 441.3 jit_solution(476243138658292207)
XLA Ops:
  7.2 0.0 reduce-scatter.7.cloned.1.call-start
  7.2 0.7 reduce-scatter.7.cloned.1.call-update
  7.9 0.0 all-gather.6.cloned.1.call-start
  7.9 71.7 %reduce-scatter.7.cloned.1.call-done = bf16[128,6144]{1,0:T(8,128)(2,1)} async-done(((bf16[512,6144]{1,0:T(8,128)(2,1)}), bf16[128,6144]{1,0:T(8,128)(2,1)}) %reduce-scatter.7.cloned.1.call-update) | async-done | bytes 1572880
  79.6 1.9 copy.14
  81.5 24.2 %all_to_all.38 = bf16[128,8,768]{0,2,1:T(8,128)(2,1)S(1)} all-to-all(bf16[128,8,768]{0,2,1:T(8,128)(2,1)S(1)} %bitcast.15), channel_id=1, replica_groups=mesh['rep'=4,'row'=4,'col'=8] {'col'}, dimensions={1} | all-to-all | bytes 3145728 | tf_op jit(solution)/shard_map/all_to_all | solution.py:11
  105.7 1.6 copy.11
  107.3 0.0 all-gather.6.cloned.1.call-update
  107.3 0.0 all-gather.4.cloned.1.call-start
  107.3 29.4 %all_to_all.39 = bf16[128,4,1536]{0,2,1:T(8,128)(2,1)S(1)} all-to-all(bf16[128,4,1536]{0,2,1:T(8,128)(2,1)S(1)} %bitcast.16), channel_id=1, replica_groups=mesh['rep'=4,'row'=4,'col'=8] {'row'}, dimensions={1} | all-to-all | bytes 3145728 | tf_op jit(solution)/shard_map/all_to_all | solution.py:10
  136.7 1.6 copy.10
  138.3 0.0 all-gather.4.cloned.1.call-update
  138.3 0.0 reduce-scatter.5.cloned.1.call-start
  138.4 44.5 %all-gather.6.cloned.1.call-done = bf16[4096,768]{1,0:T(8,128)(2,1)} async-done(((bf16[1024,768]{1,0:T(8,128)(2,1)}), bf16[4096,768]{1,0:T(8,128)(2,1)}) %all-gather.6.cloned.1.call-update) | async-done | bytes 6291472 | tf_op jit(solution)/shard_map/all_gather | solution.py:15
  182.9 6.0 %copy.12 = bf16[4,8,128,768]{3,2,0,1:T(8,128)(2,1)} copy(bf16[4,8,128,768]{3,2,1,0:T(8,128)(2,1)} %bitcast.18) | data formatting | bytes 12582912 | tf_op jit(solution)/shard_map/reshape | solution.py:17
  188.9 123.7 %all-gather.4.cloned.1.call-done = bf16[4096,1536]{1,0:T(8,128)(2,1)} async-done(((bf16[512,1536]{1,0:T(8,128)(2,1)}), bf16[4096,1536]{1,0:T(8,128)(2,1)}) %all-gather.4.cloned.1.call-update) | async-done | bytes 12582928 | tf_op jit(solution)/shard_map/all_gather | solution.py:22
  312.6 16.4 %fusion = f32[1536,768]{1,0:T(8,128)} fusion(bf16[4096,1536]{1,0:T(8,128)(2,1)} %all-gather.4.cloned.1.call-done, bf16[4096,768]{1,0:T(8,128)(2,1)} %bitcast.19), kind=kOutput, calls=%fused_computation.1 | convolution fusion | flops 9663676416 | bytes 23592960 | tf_op jit(solution)/shard_map/dot_general | solution.py:21
  328.9 0.0 reduce-scatter.5.cloned.1.call-update
  328.9 0.0 all-gather.8.cloned.1.call-start
  329.0 53.8 %reduce-scatter.5.cloned.1.call-done = f32[384,768]{1,0:T(8,128)} async-done(((f32[1536,768]{1,0:T(8,128)}), f32[384,768]{1,0:T(8,128)}) %reduce-scatter.5.cloned.1.call-update) | async-done | bytes 1179664 | tf_op jit(solution)/shard_map/reduce_scatter | solution.py:27
  382.8 0.0 all-gather.8.cloned.1.call-update
  382.8 42.9 %all-gather.8.cloned.1.call-done = f32[1536,768]{1,0:T(8,128)} async-done(((f32[384,768]{1,0:T(8,128)}), f32[1536,768]{1,0:T(8,128)}) %all-gather.8.cloned.1.call-update) | async-done | bytes 4718608 | tf_op jit(solution)/shard_map/all_gather | solution.py:28
  425.7 6.8 %multiply_add_fusion = f32[1536,768]{1,0:T(8,128)} fusion(f32[1536,768]{1,0:T(8,128)} %all-gather.8.cloned.1.call-done, f32[1536,768]{1,0:T(8,128)} %param.3), kind=kLoop, calls=%fused_computation | loop fusion | flops 3538944 | bytes 14155776 | tf_op jit(solution)/shard_map/add | solution.py:29
  432.6 2.2 copy.17
  (2 shorter events, 0.0 us)
Async XLA Ops:
  7.2 72.4 %reduce-scatter.7.cloned.1.call-start = ((), (), s32[]{:S(2)}) async-start(), calls=%async_computation.8 | async-start | bytes 7864320
  7.9 175.0 %all-gather.6.cloned.1.call-start = ((), (), s32[]{:S(2)}) async-start(), calls=%async_computation.5 | async-start | bytes 7864320 | tf_op jit(solution)/shard_map/all_gather | solution.py:15
  107.3 205.3 %all-gather.4.cloned.1.call-start = ((), (), s32[]{:S(2)}) async-start(), calls=%async_computation.4 | async-start | bytes 14155776 | tf_op jit(solution)/shard_map/all_gather | solution.py:22
  138.3 244.5 %reduce-scatter.5.cloned.1.call-start = ((), (), s32[]{:S(2)}) async-start(), calls=%async_computation.6 | async-start | bytes 5898240 | tf_op jit(solution)/shard_map/reduce_scatter | solution.py:27
  328.9 96.8 %all-gather.8.cloned.1.call-start = ((), (), s32[]{:S(2)}) async-start(), calls=%async_computation.7 | async-start | bytes 5898240 | tf_op jit(solution)/shard_map/all_gather | solution.py:28
  425.7 6.9 %copy-start = (f32[1536,768]{1,0:T(8,128)S(1)}, f32[1536,768]{1,0:T(8,128)}, u32[]{:S(2)}) copy-start(f32[1536,768]{1,0:T(8,128)} %all-gather.8.cloned.1.call-done) | copy-start | bytes 14155780
Sparse Core Ops, SparseCore 0:
  10.6 68.9 reduce-scatter.6
  107.4 75.4 all-gather.5
  185.1 127.4 all-gather.3
  329.1 53.6 reduce-scatter.4
  384.3 41.3 all-gather.7
where the time goes:
time: 442 us; the launch traced here: 441 us
  waiting for transfers between devices  337 us (76%)
  blocking collectives  53.6 us (12%)
  matrix products  16.4 us (4%)
  between operations  13.8 us (3%)
  local copies, waits for them, and re-layouts  13.3 us (3%)
  other arithmetic  6.85 us (2%)
    all_gather x1, waiting for transfers between devices, shards(): lax.all_gather(rows_panel, 'col', axis=0, tiled=True)  124 us
    unnamed x6, waiting for transfers between devices  72.4 us
    reduce_scatter x1, waiting for transfers between devices, shards(): lax.psum_scatter(partial_tile, 'rep', scatter_dimension=0, tiled=True)  53.8 us
    all_gather x1, waiting for transfers between devices, shards(): right_whole = lax.all_gather(cols_panel, 'row', axis=0, tiled=True)  44.5 us
    all_gather x1, waiting for transfers between devices, shards(): gram_tile = lax.all_gather(portion, 'rep', axis=0, tiled=True)  42.9 us
    all_to_all x1, blocking collectives, shards(): lax.all_to_all(summed, 'row', split_axis=1, concat_axis=0, tiled=True)  29.4 us
    all_to_all x1, blocking collectives, shards(): lax.all_to_all(summed, 'col', split_axis=1, concat_axis=0, tiled=True)  24.2 us
    dot_general x1, matrix products, shards(): lax.dot_general(lax.all_gather(rows_panel, 'col', axis=0, tiled=True), ri...  16.4 us
  transfers between devices with their start and end apart: 5, of which 5 were waited for; matrix products, arithmetic and copies ran while one was open for 2% of the time, Pallas kernels for 0%

commit v1 on v0

--- a/solution.py
+++ b/solution.py
@@ -2,6 +2,27 @@
 import jax.numpy as jnp
 from jax import lax
 from jax.sharding import PartitionSpec as P
+
+
+def gather_around(x, axis, dim):
+    length, here, width = (lax.axis_size(axis), lax.axis_index(axis), x.shape[dim])
+    right = [(i, (i + 1) % length) for i in range(length)]
+    downward = [(i, (i - 1) % length) for i in range(length)]
+    whole = jnp.zeros((*x.shape[:dim], length * width, *x.shape[dim + 1 :]), x.dtype)
+    whole = lax.dynamic_update_slice_in_dim(whole, x, here * width, axis=dim)
+    from_left = from_right = x
+    half = length // 2
+    for step in range(1, half + 1):
+        from_left = lax.ppermute(from_left, axis, right)
+        whole = lax.dynamic_update_slice_in_dim(
+            whole, from_left, (here - step) % length * width, axis=dim
+        )
+        if step < length - half:
+            from_right = lax.ppermute(from_right, axis, downward)
+            whole = lax.dynamic_update_slice_in_dim(
+                whole, from_right, (here + step) % length * width, axis=dim
+            )
+    return whole
 
 
 def shards(grad_parts, statistic):
@@ -12,7 +33,7 @@
     row_count = lax.axis_size("row")
     col_count = lax.axis_size("col")
     quarter = summed.shape[0]
-    right_whole = lax.all_gather(cols_panel, "row", axis=0, tiled=True)
+    right_whole = gather_around(cols_panel, "row", 0)
     right_order = (
         right_whole.reshape(row_count, col_count, quarter, -1)
         .transpose(1, 0, 2, 3)

time: 442 us -> 387 us (0.88)
  waiting for transfers between devices: 337 us -> 262 us
  local copies, waits for them, and re-layouts: 13.3 us -> 29.2 us
    all_gather x1, waiting for transfers between devices: 124 us -> 46.6 us  [shards(): lax.all_gather(rows_panel, 'col', axis=0, tiled=True)]
    ppermute x0 -> x3, waiting for transfers between devices: none -> 55.7 us  [the longest x2 55.7 us: gather_around(): from_left = lax.ppermute(from_left, axis, right)]
    all_gather x1 -> x0, waiting for transfers between devices: 44.5 us -> none  [shards(): right_whole = lax.all_gather(cols_panel, 'row', axis=0, tiled=True)]
    unnamed x4, local copies, waits for them, and re-layouts: 4.1 us -> 20 us
    all_to_all x1, blocking collectives: 24.2 us -> 31.5 us  [shards(): lax.all_to_all(summed, 'col', split_axis=1, concat_axis=0, tiled=True)]
    all_gather x1, waiting for transfers between devices: 42.9 us -> 36.9 us  [shards(): gram_tile = lax.all_gather(portion, 'rep', axis=0, tiled=True)]
    reshape x1 -> x0, local copies, waits for them, and re-layouts: 6.04 us -> none  [shards(): right_whole.reshape(row_count, col_count, quarter, -1).transpose(1, 0, 2, 3)]
    all_to_all x1, blocking collectives: 29.4 us -> 23.5 us  [shards(): lax.all_to_all(summed, 'row', split_axis=1, concat_axis=0, tiled=True)]
  transfers between devices with their start and end apart: 5 -> 7, of which waited for: 5 -> 6; matrix products, arithmetic and copies ran while one was open for 2% -> 4% of each run, Pallas kernels for 0% -> 0%
where the time goes in v1:
time: 387 us; the launch traced here: 386 us
  waiting for transfers between devices  262 us (68%)
  blocking collectives  55 us (14%)
  local copies, waits for them, and re-layouts  29.2 us (8%)
  matrix products  16.3 us (4%)
  between operations  13.8 us (4%)
  other arithmetic  7.07 us (2%)
    unnamed x5, waiting for transfers between devices  72.4 us
    ppermute x2, waiting for transfers between devices, gather_around(): from_left = lax.ppermute(from_left, axis, right)  55.7 us
    reduce_scatter x1, waiting for transfers between devices, shards(): lax.psum_scatter(partial_tile, 'rep', scatter_dimension=0, tiled=True)  50.4 us
    all_gather x1, waiting for transfers between devices, shards(): lax.all_gather(rows_panel, 'col', axis=0, tiled=True)  46.6 us
    all_gather x1, waiting for transfers between devices, shards(): gram_tile = lax.all_gather(portion, 'rep', axis=0, tiled=True)  36.9 us
    all_to_all x1, blocking collectives, shards(): lax.all_to_all(summed, 'col', split_axis=1, concat_axis=0, tiled=True)  31.5 us
    all_to_all x1, blocking collectives, shards(): lax.all_to_all(summed, 'row', split_axis=1, concat_axis=0, tiled=True)  23.5 us
    unnamed x4, local copies, waits for them, and re-layouts  20 us
  transfers between devices with their start and end apart: 7, of which 6 were waited for; matrix products, arithmetic and copies ran while one was open for 4% of the time, Pallas kernels for 0%

profile of v1, /device:TPU:1, one launch (start us, length us, event | category | flops | bytes accessed | tf_op | source)
XLA Modules:
  0.0 386.2 jit_solution(13348658719325743367)
XLA Ops:
  7.2 0.7 reduce-scatter.7.cloned.1.call-update
  7.9 71.7 %reduce-scatter.7.cloned.1.call-done = bf16[128,6144]{1,0:T(8,128)(2,1)} async-done(((bf16[512,6144]{1,0:T(8,128)(2,1)}), bf16[128,6144]{1,0:T(8,128)(2,1)}) %reduce-scatter.7.cloned.1.call-update) | async-done | bytes 1572880
  79.6 1.9 copy.25
  81.5 23.5 %all_to_all.38 = bf16[128,4,1536]{0,2,1:T(8,128)(2,1)S(1)} all-to-all(bf16[128,4,1536]{0,2,1:T(8,128)(2,1)S(1)} %bitcast.18), channel_id=1, replica_groups=mesh['rep'=4,'row'=4,'col'=8] {'row'}, dimensions={1} | all-to-all | bytes 3145728 | tf_op jit(solution)/shard_map/all_to_all | solution.py:31
  105.0 1.6 copy.20
  106.6 31.5 %all_to_all.39 = bf16[128,8,768]{0,2,1:T(8,128)(2,1)S(1)} all-to-all(bf16[128,8,768]{0,2,1:T(8,128)(2,1)S(1)} %bitcast.19), channel_id=1, replica_groups=mesh['rep'=4,'row'=4,'col'=8] {'col'}, dimensions={1} | all-to-all | bytes 3145728 | tf_op jit(solution)/shard_map/all_to_all | solution.py:32
  138.1 0.7 copy.18
  138.9 2.7 collective-permute-start.1
  141.6 25.1 %collective-permute-done = bf16[1024,768]{1,0:T(8,128)(2,1)S(1)} collective-permute-done((bf16[1024,768]{1,0:T(8,128)(2,1)S(1)}, bf16[1024,768]{1,0:T(8,128)(2,1)S(1)}, u32[]{:S(2)}, u32[]{:S(2)}) %collective-permute-start) | collective-permute-done | bytes 1572896 | tf_op jit(solution)/shard_map/ppermute | solution.py:16
  166.6 0.4 broadcast_in_dim.3
  167.1 0.2 constant_dynamic-update-slice_fusion.3
  167.2 0.2 constant_dynamic-update-slice_fusion.2
  167.4 1.6 constant_dynamic-update-slice_fusion.1
  169.0 30.6 %collective-permute-done.2 = bf16[1024,768]{1,0:T(8,128)(2,1)} collective-permute-done((bf16[1024,768]{1,0:T(8,128)(2,1)S(1)}, bf16[1024,768]{1,0:T(8,128)(2,1)}, u32[]{:S(2)}, u32[]{:S(2)}) %collective-permute-start.2) | collective-permute-done | bytes 1572896 | tf_op jit(solution)/shard_map/ppermute | solution.py:16
  199.6 1.6 constant_dynamic-update-slice_fusion
  201.2 3.0 copy.19
  204.2 46.6 %all-gather.3.cloned.1.call-done = bf16[4096,1536]{1,0:T(8,128)(2,1)} async-done(((bf16[512,1536]{1,0:T(8,128)(2,1)}), bf16[4096,1536]{1,0:T(8,128)(2,1)}) %all-gather.3.cloned.1.call-update) | async-done | bytes 12582928 | tf_op jit(solution)/shard_map/all_gather | solution.py:43
  250.8 16.3 %convolution_bitcast_fusion = f32[1536,768]{0,1:T(8,128)} fusion(bf16[4096,768]{1,0:T(8,128)(2,1)} %bitcast.21, bf16[4096,1536]{1,0:T(8,128)(2,1)} %all-gather.3.cloned.1.call-done), kind=kOutput, calls=%fused_computation.1 | convolution fusion | flops 9663676416 | bytes 23592960 | tf_op jit(solution)/shard_map/dot_general | solution.py:42
  267.2 50.4 %reduce-scatter.5.cloned.1.call-done = f32[384,768]{0,1:T(8,128)} async-done(((f32[1536,768]{0,1:T(8,128)}), f32[384,768]{0,1:T(8,128)}) %reduce-scatter.5.cloned.1.call-update) | async-done | bytes 1179664 | tf_op jit(solution)/shard_map/reduce_scatter | solution.py:48
  317.6 6.0 %copy.21 = f32[1536,768]{0,1:T(8,128)} copy(f32[1536,768]{1,0:T(8,128)} %param.3) | data formatting | bytes 9437184 | tf_op args[1]
  323.7 36.9 %all-gather.5.cloned.1.call-done = f32[1536,768]{0,1:T(8,128)} async-done(((f32[384,768]{0,1:T(8,128)}), f32[1536,768]{0,1:T(8,128)}) %all-gather.5.cloned.1.call-update) | async-done | bytes 4718608 | tf_op jit(solution)/shard_map/all_gather | solution.py:49
  360.5 7.1 %multiply_add_fusion = f32[1536,768]{0,1:T(8,128)} fusion(f32[1536,768]{0,1:T(8,128)} %all-gather.5.cloned.1.call-done, f32[1536,768]{0,1:T(8,128)} %copy.21), kind=kLoop, calls=%fused_computation | loop fusion | flops 3538944 | bytes 14155776 | tf_op jit(solution)/shard_map/add | solution.py:50
  367.6 6.0 %copy.23 = f32[1536,768]{1,0:T(8,128)} copy(f32[1536,768]{0,1:T(8,128)} %multiply_add_fusion) | data formatting | bytes 9437184
  373.6 6.0 %copy.22 = f32[1536,768]{1,0:T(8,128)} copy(f32[1536,768]{0,1:T(8,128)} %all-gather.5.cloned.1.call-done) | data formatting | bytes 9437184
  (10 shorter events, 0.3 us)
Async XLA Ops:
  7.2 72.4 %reduce-scatter.7.cloned.1.call-start = ((), (), s32[]{:S(2)}) async-start(), calls=%async_computation.7 | async-start | bytes 7864320
  7.9 242.9 %all-gather.3.cloned.1.call-start = ((), (), s32[]{:S(2)}) async-start(), calls=%async_computation.4 | async-start | bytes 14155776 | tf_op jit(solution)/shard_map/all_gather | solution.py:43
  106.5 211.0 %reduce-scatter.5.cloned.1.call-start = ((), (), s32[]{:S(2)}) async-start(), calls=%async_computation.5 | async-start | bytes 5898240 | tf_op jit(solution)/shard_map/reduce_scatter | solution.py:48
  138.8 27.8 %collective-permute-start = (bf16[1024,768]{1,0:T(8,128)(2,1)S(1)}, bf16[1024,768]{1,0:T(8,128)(2,1)S(1)}, u32[]{:S(2)}, u32[]{:S(2)}) collective-permute-start(bf16[1024,768]{1,0:T(8,128)(2,1)S(1)} %bitcast.25), channel_id=1, source_target_pairs={{0,8},{8,16},{16,24},{24,0},{1,9},{9,17},{17,25},{25,1},{2,10},{10... | collective-permute-start | bytes 4718600 | tf_op jit(solution)/shard_map/ppermute | solution.py:16
  138.9 28.5 %collective-permute-start.1 = (bf16[1024,768]{1,0:T(8,128)(2,1)S(1)}, bf16[1024,768]{1,0:T(8,128)(2,1)}, u32[]{:S(2)}, u32[]{:S(2)}) collective-permute-start(bf16[1024,768]{1,0:T(8,128)(2,1)S(1)} %bitcast.26), channel_id=1, source_target_pairs={{0,24},{8,0},{16,8},{24,16},{1,25},{9,1},{17,9},{25,17},{2,26},{10... | collective-permute-start | bytes 4718600 | tf_op jit(solution)/shard_map/ppermute | solution.py:21
  166.6 33.0 %collective-permute-start.2 = (bf16[1024,768]{1,0:T(8,128)(2,1)S(1)}, bf16[1024,768]{1,0:T(8,128)(2,1)}, u32[]{:S(2)}, u32[]{:S(2)}) collective-permute-start(bf16[1024,768]{1,0:T(8,128)(2,1)S(1)} %collective-permute-done), channel_id=1, source_target_pairs={{0,8},{8,16},{16,24},{24,0},{1,9},{9,17},{17,25},{25,1},{2,10},{10... | collective-permute-start | bytes 4718600 | tf_op jit(solution)/shard_map/ppermute | solution.py:16
  267.1 93.4 %all-gather.5.cloned.1.call-start = ((), (), s32[]{:S(2)}) async-start(), calls=%async_computation.6 | async-start | bytes 5898240 | tf_op jit(solution)/shard_map/all_gather | solution.py:49
Sparse Core Ops, SparseCore 0:
  10.6 68.9 reduce-scatter.6
  106.7 144.1 all-gather.2
  267.3 50.2 reduce-scatter.4
  319.1 41.3 all-gather.4

commit v2 on v0

--- a/solution.py
+++ b/solution.py
@@ -7,7 +7,10 @@
 def shards(grad_parts, statistic):
     own_part = grad_parts[0].astype(jnp.float32)
     summed = lax.psum_scatter(own_part.astype(jnp.bfloat16), "rep", scatter_dimension=0, tiled=True)
-    rows_panel = lax.all_to_all(summed, "row", split_axis=1, concat_axis=0, tiled=True)
+    rows_panel = jnp.concatenate(
+        lax.all_to_all(jnp.stack(jnp.split(summed, lax.axis_size("row"), axis=1)), "row", 0, 0),
+        axis=0,
+    )
     cols_panel = lax.all_to_all(summed, "col", split_axis=1, concat_axis=0, tiled=True)
     row_count = lax.axis_size("row")
     col_count = lax.axis_size("col")

time: 442 us -> 442 us (level)
    reduce_scatter x0 -> x1, waiting for transfers between devices: none -> 71.7 us  [shards(): lax.psum_scatter(own_part.astype(jnp.bfloat16), 'rep', scatter_dimension=...]
    unnamed x6 -> x5, waiting for transfers between devices: 72.4 us -> 0.75 us
  transfers between devices with their start and end apart: 5 -> 5, of which waited for: 5 -> 5; matrix products, arithmetic and copies ran while one was open for 2% -> 1% of each run, Pallas kernels for 0% -> 0%
where the time goes in v2:
time: 442 us
  waiting for transfers between devices  338 us (76%)
  blocking collectives  54.3 us (12%)
  matrix products  16.4 us (4%)
  between operations  13.8 us (3%)
  local copies, waits for them, and re-layouts  12.5 us (3%)
  other arithmetic  7.05 us (2%)
    all_gather x1, waiting for transfers between devices, shards(): lax.all_gather(rows_panel, 'col', axis=0, tiled=True)  123 us
    reduce_scatter x1, waiting for transfers between devices, shards(): lax.psum_scatter(own_part.astype(jnp.bfloat16), 'rep', scatter_dimension=...  71.7 us
    reduce_scatter x1, waiting for transfers between devices, shards(): lax.psum_scatter(partial_tile, 'rep', scatter_dimension=0, tiled=True)  53.8 us
    all_gather x1, waiting for transfers between devices, shards(): right_whole = lax.all_gather(cols_panel, 'row', axis=0, tiled=True)  45.7 us
    all_gather x1, waiting for transfers between devices, shards(): gram_tile = lax.all_gather(portion, 'rep', axis=0, tiled=True)  42.9 us
    all_to_all x1, blocking collectives, shards(): lax.all_to_all(jnp.stack(jnp.split(summed, lax.axis_size('row'), axis=1))...  29.8 us
    all_to_all x1, blocking collectives, shards(): lax.all_to_all(summed, 'col', split_axis=1, concat_axis=0, tiled=True)  24.5 us
    dot_general x1, matrix products, shards(): lax.dot_general(lax.all_gather(rows_panel, 'col', axis=0, tiled=True), ri...  16.4 us
  transfers between devices with their start and end apart: 5, of which 5 were waited for; matrix products, arithmetic and copies ran while one was open for 1% of the time, Pallas kernels for 0%

profile of v2, /device:TPU:1, one launch (start us, length us, event | category | flops | bytes accessed | tf_op | source)
XLA Modules:
  0.0 442.1 jit_solution(6368349544627946037)
XLA Ops:
  7.2 0.0 reduce-scatter.3.cloned.1.call-start
  7.2 0.7 reduce-scatter.3.cloned.1.call-update
  7.9 0.0 all-gather.6.cloned.1.call-start
  7.9 71.7 %reduce-scatter.3.cloned.1.call-done = bf16[128,6144]{1,0:T(8,128)(2,1)} async-done(((bf16[512,6144]{1,0:T(8,128)(2,1)}), bf16[128,6144]{1,0:T(8,128)(2,1)}) %reduce-scatter.3.cloned.1.call-update) | async-done | bytes 1572880 | tf_op jit(solution)/shard_map/reduce_scatter | solution.py:9
  79.6 2.6 copy.8
  82.2 24.5 %all_to_all.24 = bf16[128,8,768]{0,2,1:T(8,128)(2,1)S(1)} all-to-all(bf16[128,8,768]{0,2,1:T(8,128)(2,1)} %bitcast.25), channel_id=1, replica_groups=mesh['rep'=4,'row'=4,'col'=8] {'col'}, dimensions={1} | all-to-all | bytes 3145728 | tf_op jit(solution)/shard_map/all_to_all | solution.py:14
  106.7 1.6 copy.9
  108.2 0.0 all-gather.6.cloned.1.call-update
  108.3 0.0 all-gather.4.cloned.1.call-start
  108.3 0.1 slice_bitcast_fusion.3
  108.5 0.2 pad_maximum_fusion
  108.7 29.8 %all_to_all.25 = bf16[4,128,1536]{2,1,0:T(8,128)(2,1)} all-to-all(bf16[4,128,1536]{2,1,0:T(8,128)(2,1)S(1)} %pad_maximum_fusion), channel_id=1, replica_groups=mesh['rep'=4,'row'=4,'col'=8] {'row'}, dimensions={0} | all-to-all | bytes 3145728 | tf_op jit(solution)/shard_map/all_to_all | solution.py:11
  138.4 0.0 all-gather.4.cloned.1.call-update
  138.5 0.0 reduce-scatter.5.cloned.1.call-start
  138.5 45.7 %all-gather.6.cloned.1.call-done = bf16[4096,768]{1,0:T(8,128)(2,1)} async-done(((bf16[1024,768]{1,0:T(8,128)(2,1)}), bf16[4096,768]{1,0:T(8,128)(2,1)}) %all-gather.6.cloned.1.call-update) | async-done | bytes 6291472 | tf_op jit(solution)/shard_map/all_gather | solution.py:18
  184.2 6.0 %copy.10 = bf16[4,8,128,768]{3,2,0,1:T(8,128)(2,1)} copy(bf16[4,8,128,768]{3,2,1,0:T(8,128)(2,1)} %bitcast.20) | data formatting | bytes 12582912 | tf_op jit(solution)/shard_map/reshape | solution.py:20
  190.2 123.1 %all-gather.4.cloned.1.call-done = bf16[4096,1536]{1,0:T(8,128)(2,1)} async-done(((bf16[512,1536]{1,0:T(8,128)(2,1)}), bf16[4096,1536]{1,0:T(8,128)(2,1)}) %all-gather.4.cloned.1.call-update) | async-done | bytes 12582928 | tf_op jit(solution)/shard_map/all_gather | solution.py:25
  313.3 16.4 %fusion = f32[1536,768]{1,0:T(8,128)} fusion(bf16[4096,1536]{1,0:T(8,128)(2,1)} %all-gather.4.cloned.1.call-done, bf16[4096,768]{1,0:T(8,128)(2,1)} %bitcast.21), kind=kOutput, calls=%fused_computation.6 | convolution fusion | flops 9663676416 | bytes 23592960 | tf_op jit(solution)/shard_map/dot_general | solution.py:24
  329.7 0.0 all-gather.8.cloned.1.call-start
  329.7 53.8 %reduce-scatter.5.cloned.1.call-done = f32[384,768]{1,0:T(8,128)} async-done(((f32[1536,768]{1,0:T(8,128)}), f32[384,768]{1,0:T(8,128)}) %reduce-scatter.5.cloned.1.call-update) | async-done | bytes 1179664 | tf_op jit(solution)/shard_map/reduce_scatter | solution.py:30
  383.6 0.0 all-gather.8.cloned.1.call-update
  383.6 42.9 %all-gather.8.cloned.1.call-done = f32[1536,768]{1,0:T(8,128)} async-done(((f32[384,768]{1,0:T(8,128)}), f32[1536,768]{1,0:T(8,128)}) %all-gather.8.cloned.1.call-update) | async-done | bytes 4718608 | tf_op jit(solution)/shard_map/all_gather | solution.py:31
  426.5 6.8 %multiply_add_fusion = f32[1536,768]{1,0:T(8,128)} fusion(f32[1536,768]{1,0:T(8,128)} %all-gather.8.cloned.1.call-done, f32[1536,768]{1,0:T(8,128)} %param.3), kind=kLoop, calls=%fused_computation | loop fusion | flops 3538944 | bytes 14155776 | tf_op jit(solution)/shard_map/add | solution.py:32
  433.4 2.2 copy.12
  (5 shorter events, 0.0 us)
Async XLA Ops:
  7.2 72.4 %reduce-scatter.3.cloned.1.call-start = ((), (), s32[]{:S(2)}) async-start(), calls=%async_computation.4 | async-start | bytes 7864320 | tf_op jit(solution)/shard_map/reduce_scatter | solution.py:9
  7.9 176.3 %all-gather.6.cloned.1.call-start = ((), (), s32[]{:S(2)}) async-start(), calls=%async_computation.6 | async-start | bytes 7864320 | tf_op jit(solution)/shard_map/all_gather | solution.py:18
  82.2 26.2 %copy-start.1 = (bf16[128,6144]{1,0:T(8,128)(2,1)S(1)}, bf16[128,6144]{1,0:T(8,128)(2,1)}, u32[]{:S(2)}) copy-start(bf16[128,6144]{1,0:T(8,128)(2,1)} %reduce-scatter.3.cloned.1.call-done) | copy-start | bytes 4718596
  108.3 205.1 %all-gather.4.cloned.1.call-start = ((), (), s32[]{:S(2)}) async-start(), calls=%async_computation.5 | async-start | bytes 14155776 | tf_op jit(solution)/shard_map/all_gather | solution.py:25
  138.5 245.1 %reduce-scatter.5.cloned.1.call-start = ((), (), s32[]{:S(2)}) async-start(), calls=%async_computation.7 | async-start | bytes 5898240 | tf_op jit(solution)/shard_map/reduce_scatter | solution.py:30
  329.7 96.8 %all-gather.8.cloned.1.call-start = ((), (), s32[]{:S(2)}) async-start(), calls=%async_computation.8 | async-start | bytes 5898240 | tf_op jit(solution)/shard_map/all_gather | solution.py:31
  426.5 6.9 %copy-start = (f32[1536,768]{1,0:T(8,128)S(1)}, f32[1536,768]{1,0:T(8,128)}, u32[]{:S(2)}) copy-start(f32[1536,768]{1,0:T(8,128)} %all-gather.8.cloned.1.call-done) | copy-start | bytes 14155780
Sparse Core Ops, SparseCore 0:
  10.6 68.9 reduce-scatter.2
  108.4 75.7 all-gather.5
  185.9 127.4 all-gather.3
  329.8 53.6 reduce-scatter.4
  385.1 41.3 all-gather.7
